TPU v7x, 256 devices: a whole 4x4x8 slice. The times are simulated.
256 devices in a mesh: row: 16 (over z_lo, x, core), col: 16 (over y, z_hi).
Axes of the slice: x: 4, y: 4, z: 8 (z_hi: 4, z_lo: 2; z = z_hi * 2 + z_lo), core: 2. Of those that a mesh axis runs over, the one named last changes fastest.
Arguments:
- object_slices: float32 [4, 2, 4096, 4096], P(None, None, 'row', 'col'), may hold values from -2.5 to 2.5
- probe_wave: float32 [2, 128, 128], replicated, may hold values from -4 to 4
- offsets: int32 [16, 16, 4, 2], P('row', 'col'), may hold values from 0 to 255
- active_flags: int32 [16, 16, 4], P('row', 'col'), may hold values 0 or 1
- intensity: float32 [16, 16, 4, 128, 128], P('row', 'col'), may hold values from 0.1 to 3
Outputs:
- updated_object: float32 [4, 2, 4096, 4096], P(None, None, 'row', 'col')
- updated_probe: float32 [2, 128, 128], replicated
Inputs may be any that keep to these rules, and one draw needn't show every extreme that they name: `offsets`: each position's centre lies in its own device's tile; its window may reach into neighbouring tiles, diagonal ones included. `active_flags`: positions with flag 0 contribute nothing.
All inputs are finite; a program needn't handle non-finite values. No bound on the sum of `active_flags` on one device may be relied on, other than what follows from the above.
Results may differ from a plain program's by a relative error of at most 0.00018.
Values sent between devices are 32-bit elements; how exact they have to be, the bound alone decides.
A program may use at most 64 MiB of HBM per device.

v0:
```python
import math
import jax
import jax.numpy as jnp
from jax import lax
from jax.sharding import PartitionSpec as P

fresnel_phase = 40.0
object_step = 0.25
exact = lax.Precision.HIGHEST


def padded_2(cells, sides, width):
    for axis, dim in sides:
        count = lax.axis_size(axis)
        head = lax.slice_in_dim(cells, 0, width, axis=dim)
        tail = lax.slice_in_dim(cells, cells.shape[dim] - width, cells.shape[dim], axis=dim)
        cells = jnp.concatenate(
            [
                lax.ppermute(tail, axis, [(i, (i + 1) % count) for i in range(count)]),
                cells,
                lax.ppermute(head, axis, [((i + 1) % count, i) for i in range(count)]),
            ],
            axis=dim,
        )
    return cells


def passed_along(array, axis, by):
    length = lax.axis_size(axis)
    return lax.ppermute(array, axis, [(i, (i + by) % length) for i in range(length)])


def dft_tables(extent):
    indices = jnp.arange(extent, dtype=jnp.int32)
    angles = (indices[:, None] * indices[None, :] % extent).astype(jnp.float32) * (
        2.0 * jnp.pi / extent
    )
    norming = 1.0 / math.sqrt(extent)
    cosine = jnp.cos(angles) * norming
    sine_part = -jnp.sin(angles) * norming
    forward = jnp.stack([jnp.stack([cosine, -sine_part]), jnp.stack([sine_part, cosine])])
    backward = jnp.stack([jnp.stack([cosine, sine_part]), jnp.stack([-sine_part, cosine])])
    return (forward, backward)


def transfer(extent):
    indices = jnp.arange(extent, dtype=jnp.int32)
    frequency = ((indices + extent // 2) % extent - extent // 2).astype(jnp.float32) / extent
    phase_angle = -jnp.pi * fresnel_phase * (frequency[:, None] ** 2 + frequency[None, :] ** 2)
    return (jnp.cos(phase_angle), jnp.sin(phase_angle))


def transform(field_pair, tables, inverse):
    block = tables[1] if inverse else tables[0]
    stacked = jnp.stack(field_pair)
    left = jnp.einsum("pqjk,qbkl->pbjl", block, stacked, precision=exact)
    result = jnp.einsum("qbjk,pqkl->pbjl", left, block, precision=exact)
    return (result[0], result[1])


def complex_times(first, second):
    return (
        first[0] * second[0] - first[1] * second[1],
        first[0] * second[1] + first[1] * second[0],
    )


def conj_times(first, second):
    return (
        first[0] * second[0] + first[1] * second[1],
        first[0] * second[1] - first[1] * second[0],
    )


def propagate(field_pair, tables, kernel, adjoint):
    spectrum = transform(field_pair, tables, False)
    if adjoint:
        spectrum = conj_times(kernel, spectrum)
    else:
        spectrum = complex_times(kernel, spectrum)
    return transform(spectrum, tables, True)


def fetch_rim(object_slices, margin):
    return padded_2(object_slices, (("row", 2), ("col", 3)), margin)


def body(object_slices, probe_wave, offsets, active_flags, intensity):
    extent = probe_wave.shape[-1]
    margin = extent // 2
    layers = object_slices.shape[0]
    positions = offsets.shape[2]
    padded = fetch_rim(object_slices, margin)
    start_rows = offsets[0, 0, :, 0]
    start_cols = offsets[0, 0, :, 1]
    anchor = jnp.zeros((), jnp.int32)

    def window_at(source, top_row, left_col):
        return lax.dynamic_slice(
            source, (anchor, anchor, top_row, left_col), (layers, 2, extent, extent)
        )

    windows = jax.vmap(window_at, in_axes=(None, 0, 0))(padded, start_rows, start_cols)
    tables = dft_tables(extent)
    kernel = transfer(extent)
    flags = active_flags[0, 0].astype(jnp.float32)[:, None, None]
    observed = intensity[0, 0]
    wavefield = (
        jnp.broadcast_to(probe_wave[0], (positions, extent, extent)),
        jnp.broadcast_to(probe_wave[1], (positions, extent, extent)),
    )
    incident = []
    for layer_at in range(layers):
        incident.append(wavefield)
        transmit = (windows[:, layer_at, 0], windows[:, layer_at, 1])
        wavefield = complex_times(wavefield, transmit)
        if layer_at + 1 < layers:
            wavefield = propagate(wavefield, tables, kernel, False)
    far_field = transform(wavefield, tables, False)
    excess = flags * (far_field[0] ** 2 + far_field[1] ** 2 - observed)
    back_field = transform((excess * far_field[0], excess * far_field[1]), tables, True)
    grad_layers = [None] * layers
    for layer_at in reversed(range(layers)):
        transmit = (windows[:, layer_at, 0], windows[:, layer_at, 1])
        grad_layers[layer_at] = conj_times(incident[layer_at], back_field)
        back_field = conj_times(transmit, back_field)
        if layer_at > 0:
            back_field = propagate(back_field, tables, kernel, True)
    stacked = jnp.stack([jnp.stack(grad_pair, axis=1) for grad_pair in grad_layers], axis=1)

    def deposit(index_k, running):
        begin = (anchor, anchor, start_rows[index_k], start_cols[index_k])
        piece = stacked[index_k]
        return lax.dynamic_update_slice(
            running, lax.dynamic_slice(running, begin, piece.shape) + piece, begin
        )

    grad_pad = lax.fori_loop(0, positions, deposit, jnp.zeros_like(padded))
    from_right = passed_along(grad_pad[:, :, :, :margin], "col", -1)
    from_left = passed_along(grad_pad[:, :, :, -margin:], "col", 1)
    inner = grad_pad[:, :, :, margin:-margin]
    inner = inner.at[:, :, :, -margin:].add(from_right)
    inner = inner.at[:, :, :, :margin].add(from_left)
    from_below = passed_along(inner[:, :, :margin], "row", -1)
    from_above = passed_along(inner[:, :, -margin:], "row", 1)
    folded = inner[:, :, margin:-margin]
    folded = folded.at[:, :, -margin:].add(from_below)
    folded = folded.at[:, :, :margin].add(from_above)
    updated_object = object_slices - object_step * folded
    local_grad = jnp.stack([jnp.sum(back_field[0], axis=0), jnp.sum(back_field[1], axis=0)])
    devices = lax.axis_size("row") * lax.axis_size("col")
    factor = 1.0 / math.sqrt(positions * devices)
    summed = lax.psum(local_grad, ("row", "col"))
    updated_probe = probe_wave - factor * summed
    return (updated_object, updated_probe)


def solution(mesh):
    in_specs = (
        P(None, None, "row", "col"),
        P(),
        P("row", "col", None, None),
        P("row", "col", None),
        P("row", "col", None, None, None),
    )
    out_specs = (P(None, None, "row", "col"), P())
    return jax.shard_map(body, mesh=mesh, in_specs=in_specs, out_specs=out_specs, check_vma=False)
```

profile of v0, /device:TPU:2, one launch (start us, length us, event | category | flops | bytes accessed | tf_op | source)
XLA Modules:
  0.0 511.6 jit_solution(18418235282657406992)
XLA Ops:
  14.5 4.0 collective-permute-done
  18.4 2.4 copy.52
  20.8 2.3 copy.54
  25.1 3.3 collective-permute-start.2
  28.4 5.6 %collective-permute-start.3 = (f32[4,2,384,64]{2,3,1,0:T(8,128)S(1)}, f32[4,2,384,64]{2,3,1,0:T(8,128)S(1)}, u32[]{:S(2)}, u32[]{:S(2)}) collective-permute-start(f32[4,2,384,64]{2,3,1,0:T(8,128)S(1)} %get-tuple-element.205), channel_id=1, source_target_pairs={{1,0},{2,1},{3,2},{4,3},{5,4},{6,5},{7,6},{8,7},{9,8},{10,9},{11,1... | collective-permute-start | bytes 2359304 | tf_op jit(solution)/shard_map/ppermute | solution.py:21
  34.4 22.7 %collective-permute-done.2 = f32[4,2,384,64]{2,3,1,0:T(8,128)S(1)} collective-permute-done((f32[4,2,384,64]{2,3,1,0:T(8,128)S(1)}, f32[4,2,384,64]{2,3,1,0:T(8,128)S(1)}, u32[]{:S(2)}, u32[]{:S(2)}) %collective-permute-start.2) | collective-permute-done | bytes 786464 | tf_op jit(solution)/shard_map/ppermute | solution.py:19
  57.1 9.4 %collective-permute-done.3 = f32[4,2,384,64]{2,3,1,0:T(8,128)S(1)} collective-permute-done((f32[4,2,384,64]{2,3,1,0:T(8,128)S(1)}, f32[4,2,384,64]{2,3,1,0:T(8,128)S(1)}, u32[]{:S(2)}, u32[]{:S(2)}) %collective-permute-start.3) | collective-permute-done | bytes 786464 | tf_op jit(solution)/shard_map/ppermute | solution.py:21
  66.5 3.2 pad_maximum_fusion
  69.7 18.9 %while.19 = (s32[]{:T(128)}, f32[4,2,384,384]{2,3,1,0:T(8,128)}, s32[4,4]{1,0:T(4,128)S(1)}, f32[4,4,2,128,128]{3,4,0,2,1:T(8,128)}, s32[]{:T(128)}) while((s32[]{:T(128)}, f32[4,2,384,384]{2,3,1,0:T(8,128)}, s32[4,4]{1,0:T(4,128)S(1)}, f32[4,4,2,128,128]{3,4,0,2,1:T(8,128)}, s32[]{:T(128)}) %tuple.107), condition=%wide.while_cond.4, body=%wide.while_body.4.sunk | while | flops 2 | bytes 4194437 | solution.py:99
  70.4 2.8 constant_dynamic-slice_fusion.11
  75.1 2.8 constant_dynamic-slice_fusion.11
  79.8 2.8 constant_dynamic-slice_fusion.11
  84.5 2.8 constant_dynamic-slice_fusion.11
  111.4 2.5 broadcast_in_dim.10.clone
  113.9 64.0 %while.18 = (s32[]{:T(128)}, f32[4,2,384,384]{2,3,1,0:T(8,128)}, s32[4]{0:T(128)S(1)}, s32[4]{0:T(128)S(1)}, f32[4,4,2,128,128]{3,4,0,2,1:T(8,128)}, /*index=5*/s32[]{:T(128)}, s32[]{:T(128)}, s32[]{:T(128)}) while((s32[]{:T(128)}, f32[4,2,384,384]{2,3,1,0:T(8,128)}, s32[4]{0:T(128)S(1)}, s32[4]{0:T(128)S(1)}, ...), condition=%wide.region_1.2_spmd, body=%wide.region_0.1_spmd.sunk | while | flops 131080 | bytes 7864521 | solution.py:138
  122.2 7.7 %dynamic_update_slice.8 = f32[4,2,384,384]{2,3,1,0:T(8,128)} dynamic-update-slice(f32[4,2,384,384]{2,3,1,0:T(8,128)} %get-tuple-element.352, f32[4,2,128,128]{2,3,1,0:T(8,128)S(1)} %copy.304, s32[]{:T(128)} %constant.169.clone.1..sunk, s32[]{:T(128)} %constant.169.clone.1..sunk, s32[]{:T(128)S(6)} %select_n.167, s32[]{:T(128)S(6)} %select_n.168) | dynamic-update-slice | bytes 1048580 | tf_op jit(solution)/shard_map/while/body/eval_jaxpr/dynamic_update_slice | solution.py:134
  138.2 7.7 %dynamic_update_slice.8 = f32[4,2,384,384]{2,3,1,0:T(8,128)} dynamic-update-slice(f32[4,2,384,384]{2,3,1,0:T(8,128)} %get-tuple-element.352, f32[4,2,128,128]{2,3,1,0:T(8,128)S(1)} %copy.304, s32[]{:T(128)} %constant.169.clone.1..sunk, s32[]{:T(128)} %constant.169.clone.1..sunk, s32[]{:T(128)S(6)} %select_n.167, s32[]{:T(128)S(6)} %select_n.168) | dynamic-update-slice | bytes 1048580 | tf_op jit(solution)/shard_map/while/body/eval_jaxpr/dynamic_update_slice | solution.py:134
  154.2 7.7 %dynamic_update_slice.8 = f32[4,2,384,384]{2,3,1,0:T(8,128)} dynamic-update-slice(f32[4,2,384,384]{2,3,1,0:T(8,128)} %get-tuple-element.352, f32[4,2,128,128]{2,3,1,0:T(8,128)S(1)} %copy.304, s32[]{:T(128)} %constant.169.clone.1..sunk, s32[]{:T(128)} %constant.169.clone.1..sunk, s32[]{:T(128)S(6)} %select_n.167, s32[]{:T(128)S(6)} %select_n.168) | dynamic-update-slice | bytes 1048580 | tf_op jit(solution)/shard_map/while/body/eval_jaxpr/dynamic_update_slice | solution.py:134
  170.2 7.7 %dynamic_update_slice.8 = f32[4,2,384,384]{2,3,1,0:T(8,128)} dynamic-update-slice(f32[4,2,384,384]{2,3,1,0:T(8,128)} %get-tuple-element.352, f32[4,2,128,128]{2,3,1,0:T(8,128)S(1)} %copy.304, s32[]{:T(128)} %constant.169.clone.1..sunk, s32[]{:T(128)} %constant.169.clone.1..sunk, s32[]{:T(128)S(6)} %select_n.167, s32[]{:T(128)S(6)} %select_n.168) | dynamic-update-slice | bytes 1048580 | tf_op jit(solution)/shard_map/while/body/eval_jaxpr/dynamic_update_slice | solution.py:134
  179.4 5.3 %collective-permute-start.4 = (f32[4,2,384,64]{2,3,1,0:T(8,128)S(1)}, f32[4,2,384,64]{2,3,1,0:T(8,128)S(1)}, u32[]{:S(2)}, u32[]{:S(2)}) collective-permute-start(f32[4,2,384,64]{2,3,1,0:T(8,128)S(1)} %get-tuple-element.203), channel_id=1, source_target_pairs={{0,15},{1,0},{2,1},{3,2},{4,3},{5,4},{6,5},{7,6},{8,7},{9,8},{10,9... | collective-permute-start | bytes 2359304 | tf_op jit(solution)/shard_map/ppermute | solution.py:30
  186.8 28.9 %collective-permute-done.4 = f32[4,2,384,64]{2,3,1,0:T(8,128)S(1)} collective-permute-done((f32[4,2,384,64]{2,3,1,0:T(8,128)S(1)}, f32[4,2,384,64]{2,3,1,0:T(8,128)S(1)}, u32[]{:S(2)}, u32[]{:S(2)}) %collective-permute-start.4) | collective-permute-done | bytes 786464 | tf_op jit(solution)/shard_map/ppermute | solution.py:30
  217.0 4.1 collective-permute-done.5
  223.0 2.3 copy.116
  227.4 2.3 copy.118
  230.3 243.6 %all-reduce.2.cloned.1.call-done = f32[2,128,128]{1,2,0:T(8,128)} async-done(((f32[2,128,128]{1,2,0:T(8,128)}), f32[2,128,128]{1,2,0:T(8,128)}) %all-reduce.2.cloned.1.call-update) | async-done | bytes 131088 | tf_op jit(solution)/shard_map/psum | solution.py:153
  477.5 2.4 copy.117
  479.9 2.3 slice_add_fusion.1
  482.2 6.5 %scatter-add.16 = f32[4,2,256,256]{2,3,1,0:T(8,128)} dynamic-update-slice(f32[4,2,256,256]{2,3,1,0:T(8,128)} %slice.378, f32[4,2,64,256]{2,3,1,0:T(8,128)} %slice_add_fusion.1, s32[]{:T(128)} %constant.169.clone.1, s32[]{:T(128)} %constant.169.clone.1, s32[]{:T(128)} %constant.180.clone.1, s32[]{:T(128)} %constant.169.clone.1) | dynamic-update-slice | bytes 1048580 | tf_op jit(solution)/shard_map/scatter-add | solution.py:147
  488.7 2.4 copy.119
  492.9 5.8 %scatter-add.19 = f32[4,2,256,256]{2,3,1,0:T(8,128)} dynamic-update-slice(f32[4,2,256,256]{2,3,1,0:T(8,128)} %scatter-add.16, f32[4,2,64,256]{2,3,1,0:T(8,128)S(1)} %slice_add_fusion, s32[]{:T(128)} %constant.169.clone.1, s32[]{:T(128)} %constant.169.clone.1, s32[]{:T(128)} %constant.169.clone.1, s32[]{:T(128)} %constant.169.clone.1) | dynamic-update-slice | bytes 1048580 | tf_op jit(solution)/shard_map/scatter-add | solution.py:148
  498.7 3.2 multiply_subtract_fusion
  501.9 2.9 copy.122
  (163 shorter events, 72.1 us)
Async XLA Ops:
  7.2 466.7 %all-reduce.2.cloned.1.call-start = ((), (), s32[]{:S(2)}) async-start(), calls=%async_computation | async-start | bytes 262144 | tf_op jit(solution)/shard_map/psum | solution.py:153
  9.5 8.9 %collective-permute-start = (f32[4,2,64,256]{3,2,1,0:T(8,128)}, f32[4,2,64,256]{3,2,1,0:T(8,128)}, u32[]{:S(2)}, u32[]{:S(2)}) collective-permute-start(f32[4,2,64,256]{3,2,1,0:T(8,128)} %get-tuple-element.222), channel_id=1, source_target_pairs={{0,16},{16,32},{32,48},{48,64},{64,80},{80,96},{96,112},{112,128},... | collective-permute-start | bytes 1572872 | tf_op jit(solution)/shard_map/ppermute | solution.py:19
  9.5 11.3 %collective-permute-start.1 = (f32[4,2,64,256]{3,2,1,0:T(8,128)}, f32[4,2,64,256]{3,2,1,0:T(8,128)}, u32[]{:S(2)}, u32[]{:S(2)}) collective-permute-start(f32[4,2,64,256]{3,2,1,0:T(8,128)} %get-tuple-element.223), channel_id=1, source_target_pairs={{16,0},{32,16},{48,32},{64,48},{80,64},{96,80},{112,96},{128,112},... | collective-permute-start | bytes 1572872 | tf_op jit(solution)/shard_map/ppermute | solution.py:21
  11.2 2.0 copy-start.8
  11.2 2.2 copy-start.6
  11.2 2.5 copy-start.7
  11.2 3.2 copy-start.9
  13.2 53.3 %copy-start = (f32[4,2,256,256]{2,3,1,0:T(8,128)}, f32[4,2,256,256]{2,3,1,0:T(8,128)S(1)}, u32[]{:S(2)}) copy-start(f32[4,2,256,256]{2,3,1,0:T(8,128)S(1)} %copy.120) | copy-start | bytes 6291460
  23.1 43.4 %copy-start.2 = (f32[4,2,64,256]{2,3,1,0:T(8,128)S(1)}, f32[4,2,64,256]{2,3,1,0:T(8,128)}, u32[]{:S(2)}) copy-start(f32[4,2,64,256]{2,3,1,0:T(8,128)} %copy.52) | copy-start | bytes 1572868
  23.1 43.4 %copy-start.3 = (f32[4,2,64,256]{2,3,1,0:T(8,128)S(1)}, f32[4,2,64,256]{2,3,1,0:T(8,128)}, u32[]{:S(2)}) copy-start(f32[4,2,64,256]{2,3,1,0:T(8,128)} %copy.54) | copy-start | bytes 1572868
  25.1 32.0 %collective-permute-start.2 = (f32[4,2,384,64]{2,3,1,0:T(8,128)S(1)}, f32[4,2,384,64]{2,3,1,0:T(8,128)S(1)}, u32[]{:S(2)}, u32[]{:S(2)}) collective-permute-start(f32[4,2,384,64]{2,3,1,0:T(8,128)S(1)} %get-tuple-element.204), channel_id=1, source_target_pairs={{0,1},{1,2},{2,3},{3,4},{4,5},{5,6},{6,7},{7,8},{8,9},{9,10},{10,1... | collective-permute-start | bytes 2359304 | tf_op jit(solution)/shard_map/ppermute | solution.py:19
  28.4 38.1 %collective-permute-start.3 = (f32[4,2,384,64]{2,3,1,0:T(8,128)S(1)}, f32[4,2,384,64]{2,3,1,0:T(8,128)S(1)}, u32[]{:S(2)}, u32[]{:S(2)}) collective-permute-start(f32[4,2,384,64]{2,3,1,0:T(8,128)S(1)} %get-tuple-element.205), channel_id=1, source_target_pairs={{1,0},{2,1},{3,2},{4,3},{5,4},{6,5},{7,6},{8,7},{9,8},{10,9},{11,1... | collective-permute-start | bytes 2359304 | tf_op jit(solution)/shard_map/ppermute | solution.py:21
  91.0 1.6 copy-start.4
  109.1 0.8 copy-start.5
  179.4 36.3 %collective-permute-start.4 = (f32[4,2,384,64]{2,3,1,0:T(8,128)S(1)}, f32[4,2,384,64]{2,3,1,0:T(8,128)S(1)}, u32[]{:S(2)}, u32[]{:S(2)}) collective-permute-start(f32[4,2,384,64]{2,3,1,0:T(8,128)S(1)} %get-tuple-element.203), channel_id=1, source_target_pairs={{0,15},{1,0},{2,1},{3,2},{4,3},{5,4},{6,5},{7,6},{8,7},{9,8},{10,9... | collective-permute-start | bytes 2359304 | tf_op jit(solution)/shard_map/ppermute | solution.py:30
  184.7 36.4 %collective-permute-start.5 = (f32[4,2,384,64]{2,3,1,0:T(8,128)S(1)}, f32[4,2,384,64]{2,3,1,0:T(8,128)S(1)}, u32[]{:S(2)}, u32[]{:S(2)}) collective-permute-start(f32[4,2,384,64]{2,3,1,0:T(8,128)S(1)} %get-tuple-element.202), channel_id=1, source_target_pairs={{0,1},{1,2},{2,3},{3,4},{4,5},{5,6},{6,7},{7,8},{8,9},{9,10},{10,1... | collective-permute-start | bytes 2359304 | tf_op jit(solution)/shard_map/ppermute | solution.py:30
  225.3 252.1 %collective-permute-start.6 = (f32[4,2,64,256]{3,2,1,0:T(8,128)}, f32[4,2,64,256]{3,2,1,0:T(8,128)}, u32[]{:S(2)}, u32[]{:S(2)}) collective-permute-start(f32[4,2,64,256]{3,2,1,0:T(8,128)} %copy.116), channel_id=1, source_target_pairs={{0,240},{16,0},{32,16},{48,32},{64,48},{80,64},{96,80},{112,96},{1... | collective-permute-start | bytes 1572872 | tf_op jit(solution)/shard_map/ppermute | solution.py:30
  229.8 258.9 %collective-permute-start.7 = (f32[4,2,64,256]{3,2,1,0:T(8,128)}, f32[4,2,64,256]{3,2,1,0:T(8,128)}, u32[]{:S(2)}, u32[]{:S(2)}) collective-permute-start(f32[4,2,64,256]{3,2,1,0:T(8,128)} %copy.118), channel_id=1, source_target_pairs={{0,16},{16,32},{32,48},{48,64},{64,80},{80,96},{96,112},{112,128},... | collective-permute-start | bytes 1572872 | tf_op jit(solution)/shard_map/ppermute | solution.py:30
  491.0 7.6 %copy-start.1 = (f32[4,2,256,256]{2,3,1,0:T(8,128)S(1)}, f32[4,2,256,256]{2,3,1,0:T(8,128)}, u32[]{:S(2)}) copy-start(f32[4,2,256,256]{2,3,1,0:T(8,128)} %copy-done) | copy-start | bytes 6291460
Sparse Core Ops, SparseCore 0:
  227.4 246.3 all-reduce.1
where the time goes:
time: 515 us; the launch traced here: 512 us
  waiting for transfers between devices  313 us (61%)
  local copies, waits for them, and re-layouts  113 us (22%)
  other arithmetic  21.8 us (4%)
  matrix products  17.7 us (3%)
  starting transfers between devices  16.5 us (3%)
  loops' own time  15.5 us (3%)
  between operations  14.6 us (3%)
    psum x1, waiting for transfers between devices, body(): summed = lax.psum(local_grad, ('row', 'col'))  244 us
    ppermute x4, waiting for transfers between devices, passed_along(): lax.ppermute(array, axis, [(i, (i + by) % length) for i in range(length)])  33 us
    dynamic_update_slice x8, local copies, waits for them, and re-layouts, deposit(): lax.dynamic_update_slice(running, lax.dynamic_slice(running, begin, piece...  31.6 us
    ppermute x2, waiting for transfers between devices, padded_2(): lax.ppermute(tail, axis, [(i, (i + 1) % count) for i in range(count)])  26.7 us
    gather x24, local copies, waits for them, and re-layouts  18.8 us
    another operation x1, loops' own time, body(): grad_pad = lax.fori_loop(0, positions, deposit, jnp.zeros_like(padded))  15.4 us
  transfers between devices with their start and end apart: 9, of which 6 were waited for; matrix products, arithmetic and copies ran while one was open for 6% of the time, Pallas kernels for 0%

commit v1 on v0

--- a/solution.py
+++ b/solution.py
@@ -1,3 +1,4 @@
+import functools
 import math
 import jax
 import jax.numpy as jnp
@@ -7,6 +8,14 @@
 fresnel_phase = 40.0
 object_step = 0.25
 exact = lax.Precision.HIGHEST
+
+
+def wrap_the_gates(piece_in, axis_key):
+    main = lax.all_gather(piece_in, axis_name=axis_key)
+    return jnp.sum(main, axis=0)
+
+
+test_face_now = functools.partial(wrap_the_gates, axis_key=("row", "col"))
 
 
 def padded_2(cells, sides, width):
@@ -150,7 +159,7 @@
     local_grad = jnp.stack([jnp.sum(back_field[0], axis=0), jnp.sum(back_field[1], axis=0)])
     devices = lax.axis_size("row") * lax.axis_size("col")
     factor = 1.0 / math.sqrt(positions * devices)
-    summed = lax.psum(local_grad, ("row", "col"))
+    summed = test_face_now(local_grad)
     updated_probe = probe_wave - factor * summed
     return (updated_object, updated_probe)
 

time: 515 us -> 910 us (1.77); the launches traced: 512 us -> 895 us
  waiting for transfers between devices: 313 us -> 690 us
  other arithmetic: 21.8 us -> 32.7 us
    all_gather x0 -> x1, waiting for transfers between devices: none -> 605 us  [wrap_the_gates(): main = lax.all_gather(piece_in, axis_name=axis_key)]
    psum x1 -> x0, waiting for transfers between devices: 244 us -> none  [body(): summed = lax.psum(local_grad, ('row', 'col'))]
    ppermute x2, waiting for transfers between devices: 9.39 us -> 36.7 us  [padded_2(): lax.ppermute(head, axis, [((i + 1) % count, i) for i in range(count)])]
    ppermute x2, waiting for transfers between devices: 26.7 us -> 6.08 us  [padded_2(): lax.ppermute(tail, axis, [(i, (i + 1) % count) for i in range(count)])]
    reduce_sum x0 -> x1, other arithmetic: none -> 12.3 us  [wrap_the_gates(): return jnp.sum(main, axis=0)]
    ppermute x4, waiting for transfers between devices: 33 us -> 42.3 us  [passed_along(): lax.ppermute(array, axis, [(i, (i + by) % length) for i in range(length)])]
  transfers between devices with their start and end apart: 9 -> 9, of which waited for: 6 -> 7; matrix products, arithmetic and copies ran while one was open for 6% -> 11% of each run, Pallas kernels for 0% -> 0%
where the time goes in v1:
time: 910 us; the launch traced here: 895 us
  waiting for transfers between devices  690 us (76%)
  local copies, waits for them, and re-layouts  112 us (12%)
  other arithmetic  32.7 us (4%)
  matrix products  17.7 us (2%)
  loops' own time  15.3 us (2%)
  between operations  14.7 us (2%)
  starting transfers between devices  12.8 us (1%)
    all_gather x1, waiting for transfers between devices, wrap_the_gates(): main = lax.all_gather(piece_in, axis_name=axis_key)  605 us
    ppermute x4, waiting for transfers between devices, passed_along(): lax.ppermute(array, axis, [(i, (i + by) % length) for i in range(length)])  42.3 us
    ppermute x2, waiting for transfers between devices, padded_2(): lax.ppermute(head, axis, [((i + 1) % count, i) for i in range(count)])  36.7 us
    dynamic_update_slice x8, local copies, waits for them, and re-layouts, deposit(): lax.dynamic_update_slice(running, lax.dynamic_slice(running, begin, piece...  31.8 us
    gather x24, local copies, waits for them, and re-layouts  18.5 us
  transfers between devices with their start and end apart: 9, of which 7 were waited for; matrix products, arithmetic and copies ran while one was open for 11% of the time, Pallas kernels for 0%

profile of v1, /device:TPU:2, one launch (start us, length us, event | category | flops | bytes accessed | tf_op | source)
XLA Modules:
  0.0 895.5 jit_solution(6607399223395295020)
XLA Ops:
  13.1 3.4 collective-permute-done.1
  16.5 2.4 copy.53
  19.0 2.4 copy.51
  23.4 8.7 collective-permute-start.3
  32.5 33.3 %collective-permute-done.3 = f32[4,2,384,64]{2,3,1,0:T(8,128)S(1)} collective-permute-done((f32[4,2,384,64]{2,3,1,0:T(8,128)S(1)}, f32[4,2,384,64]{2,3,1,0:T(8,128)S(1)}, u32[]{:S(2)}, u32[]{:S(2)}) %collective-permute-start.3) | collective-permute-done | bytes 786464 | tf_op jit(solution)/shard_map/ppermute | solution.py:30
  65.8 6.0 collective-permute-done.2
  71.8 3.2 pad_maximum_fusion
  75.0 18.6 %while.19 = (s32[]{:T(128)}, f32[4,2,384,384]{2,3,1,0:T(8,128)}, s32[4,4]{1,0:T(4,128)S(1)}, f32[4,4,2,128,128]{3,4,0,2,1:T(8,128)}, s32[]{:T(128)}) while((s32[]{:T(128)}, f32[4,2,384,384]{2,3,1,0:T(8,128)}, s32[4,4]{1,0:T(4,128)S(1)}, f32[4,4,2,128,128]{3,4,0,2,1:T(8,128)}, s32[]{:T(128)}) %tuple.107), condition=%wide.while_cond.4, body=%wide.while_body.4.sunk | while | flops 2 | bytes 4194437 | solution.py:108
  75.6 2.7 constant_dynamic-slice_fusion.11
  80.3 2.7 constant_dynamic-slice_fusion.11
  84.9 2.7 constant_dynamic-slice_fusion.11
  89.5 2.7 constant_dynamic-slice_fusion.11
  117.3 2.6 broadcast_in_dim.10.clone
  119.9 64.3 %while.18 = (s32[]{:T(128)}, f32[4,2,384,384]{2,3,1,0:T(8,128)}, s32[4]{0:T(128)S(1)}, s32[4]{0:T(128)S(1)}, f32[4,4,2,128,128]{3,4,0,2,1:T(8,128)}, /*index=5*/s32[]{:T(128)}, s32[]{:T(128)}, s32[]{:T(128)}) while((s32[]{:T(128)}, f32[4,2,384,384]{2,3,1,0:T(8,128)}, s32[4]{0:T(128)S(1)}, s32[4]{0:T(128)S(1)}, ...), condition=%wide.region_1.2_spmd, body=%wide.region_0.1_spmd.sunk | while | flops 131080 | bytes 7864521 | solution.py:147
  128.3 7.8 dynamic_update_slice.8
  144.3 7.7 dynamic_update_slice.8
  160.4 7.8 dynamic_update_slice.8
  176.5 7.8 dynamic_update_slice.8
  186.1 2.6 collective-permute-start.5
  190.9 38.0 %collective-permute-done.4 = f32[4,2,384,64]{2,3,1,0:T(8,128)S(1)} collective-permute-done((f32[4,2,384,64]{2,3,1,0:T(8,128)S(1)}, f32[4,2,384,64]{2,3,1,0:T(8,128)S(1)}, u32[]{:S(2)}, u32[]{:S(2)}) %collective-permute-start.4) | collective-permute-done | bytes 786464 | tf_op jit(solution)/shard_map/ppermute | solution.py:39
  232.0 2.3 copy.115
  234.3 2.3 copy.117
  239.1 4.3 collective-permute-done.6
  243.4 2.4 copy.116
  245.8 2.3 slice_add_fusion.1
  248.1 6.5 scatter-add.16
  254.6 2.4 copy.118
  258.8 5.8 scatter-add.19
  264.6 3.2 multiply_subtract_fusion
  267.8 2.9 copy.121
  270.7 605.0 %all-gather.3.cloned.1.call-done = f32[512,128,128]{2,1,0:T(8,128)} async-done(((f32[2,128,128]{2,1,0:T(8,128)}), f32[512,128,128]{2,1,0:T(8,128)}) %all-gather.3.cloned.1.call-update) | async-done | bytes 33554448 | tf_op jit(solution)/shard_map/all_gather | solution.py:14
  875.7 12.3 %reduce_sum.29 = f32[2,128,128]{2,1,0:T(8,128)S(1)} reduce(f32[256,2,128,128]{3,2,1,0:T(8,128)} %bitcast.518, f32[]{:T(128)} %constant.170.clone.1), dimensions={0}, to_apply=%region_4.5 | reduce | flops 8355840 | bytes 33685508 | tf_op jit(solution)/shard_map/reduce_sum | solution.py:15
  (173 shorter events, 69.4 us)
Async XLA Ops:
  7.2 868.5 %all-gather.3.cloned.1.call-start = ((), (), s32[]{:S(2)}) async-start(), calls=%async_computation | async-start | bytes 33685504 | tf_op jit(solution)/shard_map/all_gather | solution.py:14
  9.5 7.0 collective-permute-start.1
  9.5 2.5 copy-start.12
  9.5 2.6 copy-start.13
  9.5 2.8 copy-start.10
  9.5 9.5 %collective-permute-start = (f32[4,2,64,256]{3,2,1,0:T(8,128)}, f32[4,2,64,256]{3,2,1,0:T(8,128)}, u32[]{:S(2)}, u32[]{:S(2)}) collective-permute-start(f32[4,2,64,256]{3,2,1,0:T(8,128)} %get-tuple-element.222), channel_id=1, source_target_pairs={{0,16},{16,32},{32,48},{48,64},{64,80},{80,96},{96,112},{112,128},... | collective-permute-start | bytes 1572872 | tf_op jit(solution)/shard_map/ppermute | solution.py:28
  11.9 59.8 %copy-start = (f32[4,2,256,256]{2,3,1,0:T(8,128)}, f32[4,2,256,256]{2,3,1,0:T(8,128)S(1)}, u32[]{:S(2)}) copy-start(f32[4,2,256,256]{2,3,1,0:T(8,128)S(1)} %copy.119) | copy-start | bytes 6291460
  12.4 81.1 %copy-start.6 = (f32[128,128]{0,1:T(8,128)}, f32[128,128]{0,1:T(8,128)S(1)}, u32[]{:S(2)}) copy-start(f32[128,128]{0,1:T(8,128)S(1)} %copy.62) | copy-start | bytes 196612
  12.5 81.0 %copy-start.8 = (f32[128,128]{0,1:T(8,128)}, f32[128,128]{0,1:T(8,128)S(1)}, u32[]{:S(2)}) copy-start(f32[128,128]{0,1:T(8,128)S(1)} %copy.50) | copy-start | bytes 196612
  21.4 10.7 %copy-start.14 = (s32[1,1,4]{2,1,0:T(1,128)S(1)}, s32[1,1,4]{2,1,0:T(1,128)}, u32[]{:S(2)}) copy-start(s32[1,1,4]{2,1,0:T(1,128)} %param.18) | copy-start | bytes 52
  21.4 50.4 %copy-start.2 = (f32[4,2,64,256]{2,3,1,0:T(8,128)S(1)}, f32[4,2,64,256]{2,3,1,0:T(8,128)}, u32[]{:S(2)}) copy-start(f32[4,2,64,256]{2,3,1,0:T(8,128)} %copy.53) | copy-start | bytes 1572868
  21.4 50.4 %copy-start.3 = (f32[4,2,64,256]{2,3,1,0:T(8,128)S(1)}, f32[4,2,64,256]{2,3,1,0:T(8,128)}, u32[]{:S(2)}) copy-start(f32[4,2,64,256]{2,3,1,0:T(8,128)} %copy.51) | copy-start | bytes 1572868
  23.4 42.4 %collective-permute-start.3 = (f32[4,2,384,64]{2,3,1,0:T(8,128)S(1)}, f32[4,2,384,64]{2,3,1,0:T(8,128)S(1)}, u32[]{:S(2)}, u32[]{:S(2)}) collective-permute-start(f32[4,2,384,64]{2,3,1,0:T(8,128)S(1)} %get-tuple-element.205), channel_id=1, source_target_pairs={{1,0},{2,1},{3,2},{4,3},{5,4},{6,5},{7,6},{8,7},{9,8},{10,9},{11,1... | collective-permute-start | bytes 2359304 | tf_op jit(solution)/shard_map/ppermute | solution.py:30
  32.1 39.7 %collective-permute-start.2 = (f32[4,2,384,64]{2,3,1,0:T(8,128)S(1)}, f32[4,2,384,64]{2,3,1,0:T(8,128)S(1)}, u32[]{:S(2)}, u32[]{:S(2)}) collective-permute-start(f32[4,2,384,64]{2,3,1,0:T(8,128)S(1)} %get-tuple-element.204), channel_id=1, source_target_pairs={{0,1},{1,2},{2,3},{3,4},{4,5},{5,6},{6,7},{7,8},{8,9},{9,10},{10,1... | collective-permute-start | bytes 2359304 | tf_op jit(solution)/shard_map/ppermute | solution.py:28
  95.9 1.6 copy-start.4
  114.7 1.0 copy-start.5
  114.8 1.0 copy-start.7
  114.8 1.0 copy-start.9
  185.7 43.1 %collective-permute-start.4 = (f32[4,2,384,64]{2,3,1,0:T(8,128)S(1)}, f32[4,2,384,64]{2,3,1,0:T(8,128)S(1)}, u32[]{:S(2)}, u32[]{:S(2)}) collective-permute-start(f32[4,2,384,64]{2,3,1,0:T(8,128)S(1)} %get-tuple-element.203), channel_id=1, source_target_pairs={{0,15},{1,0},{2,1},{3,2},{4,3},{5,4},{6,5},{7,6},{8,7},{9,8},{10,9... | collective-permute-start | bytes 2359304 | tf_op jit(solution)/shard_map/ppermute | solution.py:39
  186.1 44.0 %collective-permute-start.5 = (f32[4,2,384,64]{2,3,1,0:T(8,128)S(1)}, f32[4,2,384,64]{2,3,1,0:T(8,128)S(1)}, u32[]{:S(2)}, u32[]{:S(2)}) collective-permute-start(f32[4,2,384,64]{2,3,1,0:T(8,128)S(1)} %get-tuple-element.202), channel_id=1, source_target_pairs={{0,1},{1,2},{2,3},{3,4},{4,5},{5,6},{6,7},{7,8},{8,9},{9,10},{10,1... | collective-permute-start | bytes 2359304 | tf_op jit(solution)/shard_map/ppermute | solution.py:39
  234.3 9.1 %collective-permute-start.6 = (f32[4,2,64,256]{3,2,1,0:T(8,128)}, f32[4,2,64,256]{3,2,1,0:T(8,128)}, u32[]{:S(2)}, u32[]{:S(2)}) collective-permute-start(f32[4,2,64,256]{3,2,1,0:T(8,128)} %copy.115), channel_id=1, source_target_pairs={{0,240},{16,0},{32,16},{48,32},{64,48},{80,64},{96,80},{112,96},{1... | collective-permute-start | bytes 1572872 | tf_op jit(solution)/shard_map/ppermute | solution.py:39
  236.7 17.9 %collective-permute-start.7 = (f32[4,2,64,256]{3,2,1,0:T(8,128)}, f32[4,2,64,256]{3,2,1,0:T(8,128)}, u32[]{:S(2)}, u32[]{:S(2)}) collective-permute-start(f32[4,2,64,256]{3,2,1,0:T(8,128)} %copy.117), channel_id=1, source_target_pairs={{0,16},{16,32},{32,48},{48,64},{64,80},{80,96},{96,112},{112,128},... | collective-permute-start | bytes 1572872 | tf_op jit(solution)/shard_map/ppermute | solution.py:39
  257.0 7.6 copy-start.1
  875.7 12.3 %copy-start.11 = (f32[2,128,128]{2,1,0:T(8,128)S(1)}, f32[2,128,128]{2,1,0:T(8,128)}, u32[]{:S(2)}) copy-start(f32[2,128,128]{2,1,0:T(8,128)} %param.16) | copy-start | bytes 393220
Sparse Core Ops, SparseCore 0:
  115.7 759.9 all-gather.2
